TPU v7x, 8 devices: a whole 2x2x1 slice. The times are simulated.
8 devices in a mesh: dp: 2 (over z, y), cp: 4 (over x, core).
Axes of the slice: x: 2, y: 2, z: 1, core: 2. Of those that a mesh axis runs over, the one named last changes fastest.
Arguments:
- latents: bfloat16 [32, 64, 64, 16], P('dp', 'cp'), parts along dimension 0
- w_in: bfloat16 [3, 3, 16, 512], replicated
- b_in: bfloat16 [512], replicated
- w_conv: bfloat16 [4, 3, 3, 512, 512], replicated
- b_conv: bfloat16 [4, 512], replicated
- gn_scale: bfloat16 [5, 512], replicated
- gn_shift: bfloat16 [5, 512], replicated
- w_attn: bfloat16 [4, 512, 512], replicated
- b_attn: bfloat16 [4, 512], replicated
Outputs:
- output: bfloat16 [32, 64, 64, 512], P('dp', 'cp'), parts along dimension 0
There are 2 independent parts. A program takes and returns all parts, laid end to end along the dimension named above; an argument that names none is the same for every part.
All inputs are finite; a program needn't handle non-finite values.
Results may differ from a plain program's by a relative error of at most 0.0157452.
Values are sent between devices in bfloat16 or wider.
A program may use at most 1 GiB of HBM per device.

v0:
```python
import functools

import jax
import jax.numpy as jnp
import numpy as np
from jax import lax
from jax.experimental import pallas as pl
from jax.experimental.pallas import tpu as pltpu
from jax.sharding import PartitionSpec as P


GROUPS = 32
GN_EPS = 1e-6
LANES = 128
BLOCK_ROWS = 8
F32 = jnp.float32
BF16 = jnp.bfloat16


def sample_kernel(sample, me_ref, x_hbm, w_in_ref, b_in_ref, w_conv_hbm, b_conv_ref, gn_scale_ref, gn_shift_ref,
                  w_attn_hbm, w_key_hbm, b_attn_ref, b_key_ref, far_out, cross_out, t_out, h_out, coef_out,
                  w_conv, w_attn, h, t, kt, v, s_buf, p_buf, o_buf, o_raw, m_buf, l_buf, small, params, sems):
    n_dev = h.shape[0] // far_out.shape[0]
    n_rows, width, chan = h.shape
    tokens = n_rows * width
    blk = BLOCK_ROWS * width
    n_blk = n_rows // BLOCK_ROWS
    count = tokens * (chan // GROUPS)
    n_cols = w_in_ref.shape[0]
    stat, coef = small.at[0:2], small.at[2:4]
    acc_a, acc_b = s_buf.at[:, 0:chan], s_buf.at[:, chan:2 * chan]
    lhs_rows = 3 * (BLOCK_ROWS + 2) * width
    buf_a, buf_b = v.at[0:lhs_rows], v.at[tokens // 2:tokens // 2 + lhs_rows]

    def conv_copy(idx):
        return pltpu.make_async_copy(w_conv_hbm.at[idx], w_conv.at[idx], sems.at[idx])

    attn_copies = [pltpu.make_async_copy(w_key_hbm if i == 1 else w_attn_hbm.at[i], w_attn.at[i], sems.at[6 + i]) for i in range(4)]
    me = me_ref[0]
    band = n_rows // n_dev
    half = n_rows // 2
    own_row = (me // (n_dev // 2)) * half
    far_row = half - own_row
    for i, ref in enumerate((gn_scale_ref, gn_shift_ref, b_conv_ref, b_attn_ref)):
        val = ref[...].astype(F32)
        for k in range(val.shape[0]):
            params[i, k] = val[k:k + 1]
    gn_scale, gn_shift, b_conv, b_attn = (params.at[i] for i in range(4))
    x_copy = pltpu.make_async_copy(x_hbm.at[sample], p_buf.at[0:n_cols, :], sems.at[5])
    x_copy.start()
    conv_copy(0).start()
    conv_copy(1).start()
    for copy in attn_copies:
        copy.start()
    conv_copy(2).start()
    conv_copy(3).start()

    def zero_stats():
        stat[...] = jnp.zeros((2, 8, chan), F32)

    def finish(get, put, live):
        for col in range(0, chan, LANES):
            tot = jnp.zeros((8, LANES), F32)
            tot_sq = jnp.zeros((8, LANES), F32)
            for r in range(BLOCK_ROWS):
                val = get(r, col).astype(BF16)
                put(r, col, val)
                val = val.astype(F32).reshape(width // 8, 8, LANES)
                tot = tot + jnp.sum(val, axis=0)
                tot_sq = tot_sq + jnp.sum(val * val, axis=0)
            if live is not None:
                tot = jnp.where(live, tot, 0.0)
                tot_sq = jnp.where(live, tot_sq, 0.0)
            stat[0, :, col:col + LANES] += tot
            stat[1, :, col:col + LANES] += tot_sq

    def set_coefs(idx, half):
        lane = lax.broadcasted_iota(jnp.int32, (8, chan), 1)

        def group_sum(part):
            tot = jnp.broadcast_to(jnp.sum(part, axis=0, keepdims=True), (8, chan))
            for step in (1, 2, 4, 8):
                above = pltpu.roll(tot, chan - step, 1)
                below = pltpu.roll(tot, step, 1)
                tot = tot + jnp.where((lane & step) == 0, above, below)
            return tot

        mean = group_sum(stat[0]) * (1.0 / count)
        var = jnp.maximum(group_sum(stat[1]) * (1.0 / count) - mean * mean, 0.0)
        gain = gn_scale[idx] * lax.rsqrt(var + GN_EPS)
        shift = gn_shift[idx] - mean * gain
        coef[0] = gain * half
        coef[1] = shift * half

    zero_stats()

    def conv_in_step(b, carry):
        lhs = p_buf[0:n_cols, pl.ds(pl.multiple_of(b * blk, blk), blk)]
        acc_a[...] = lax.dot_general(lhs, w_in_ref[...], (((0,), (0,)), ((), ())), preferred_element_type=F32)

        def get(r, col):
            return acc_a[r * width:(r + 1) * width, col:col + LANES] + b_in_ref[0:1, col:col + LANES]

        def put(r, col, val):
            h[b * BLOCK_ROWS + r, :, col:col + LANES] = val

        finish(get, put, None)
        return carry

    x_copy.wait()
    lax.fori_loop(0, n_blk, conv_in_step, 0)

    def prep(src, buf, b, base):
        for r in range(BLOCK_ROWS + 2):
            row = base + b * BLOCK_ROWS + (r - 1)
            row_c = jnp.clip(row, 0, n_rows - 1)
            live = (row >= 0) & (row < n_rows) if r in (0, BLOCK_ROWS + 1) else None
            activate_row(src, row_c, coef, buf, r, live)

    def conv_dots(buf, acc, idx):
        dots_of(buf, w_conv.at[idx], acc)

    def conv_finish(acc, dst, idx, b, base, residual, live):
        row0 = base + jnp.maximum(b, 0) * BLOCK_ROWS

        def get(r, col):
            val = acc[r * width:(r + 1) * width, col:col + LANES] + b_conv[idx, 0:1, col:col + LANES]
            if residual:
                old = dst[row0 + r, :, col:col + LANES].astype(F32)
                val = old + val
                if live is not None:
                    val = jnp.where(live, val, old)
            return val

        def put(r, col, val):
            dst[row0 + r, :, col:col + LANES] = val

        finish(get, put, live)

    def conv_pass(src, dst, idx, residual, base, pairs):
        zero_stats()
        prep(src, buf_a, 0, base)
        conv_copy(idx).wait()

        def pair(j, carry):
            conv_dots(buf_a, acc_a, idx)
            prep(src, buf_b, 2 * j + 1, base)
            conv_finish(acc_b, dst, idx, 2 * j - 1, base, residual, j > 0)
            conv_dots(buf_b, acc_b, idx)
            prep(src, buf_a, 2 * j + 2, base)
            conv_finish(acc_a, dst, idx, 2 * j, base, residual, None)
            return carry

        lax.fori_loop(0, pairs, pair, 0)
        conv_finish(acc_b, dst, idx, 2 * pairs - 1, base, residual, None)

    q = t.reshape(tokens, chan)
    kv_chunk = 512
    n_chunk = tokens // kv_chunk
    exp_scale = float(chan ** -0.5 * np.log2(np.e))

    def project(b, carry):
        norm = h[pl.ds(b * BLOCK_ROWS, BLOCK_ROWS)].reshape(blk, chan).astype(F32) * coef[0, 0:1, :] + coef[1, 0:1, :]
        norm = norm.astype(BF16)
        rows = pl.ds(pl.multiple_of(b * blk, blk), blk)
        q[rows, :] = (jnp.dot(norm, w_attn[0], preferred_element_type=F32) + b_attn[0]).astype(BF16)
        v[rows, :] = (jnp.dot(norm, w_attn[2], preferred_element_type=F32) + b_attn[2]).astype(BF16)
        keys = lax.dot_general(w_attn[1], norm, (((1,), (1,)), ((), ())), preferred_element_type=F32)
        kt[:, pl.ds(pl.multiple_of(b * blk, blk), blk)] = (keys + b_key_ref[...]).astype(BF16)
        return carry

    def score_chunk(q_val, c):
        val = jnp.dot(q_val, kt[:, c * kv_chunk:(c + 1) * kv_chunk], preferred_element_type=F32)
        s_buf[:, c * kv_chunk:(c + 1) * kv_chunk] = val
        for r in range(BLOCK_ROWS):
            rows = slice(r * width, (r + 1) * width)
            top = val[rows, 0:LANES]
            for col in range(LANES, kv_chunk, LANES):
                top = jnp.maximum(top, val[rows, col:col + LANES])
            m_buf[0, rows, :] = top if c == 0 else jnp.maximum(m_buf[0, rows, :], top)

    def prob_chunk(c):
        for r in range(BLOCK_ROWS):
            rows = slice(r * width, (r + 1) * width)
            m_scaled = m_buf[1, rows, :]
            tot = None
            for col in range(c * kv_chunk, (c + 1) * kv_chunk, LANES):
                val = jnp.exp2(s_buf[rows, col:col + LANES] * exp_scale - m_scaled)
                p_buf[rows, col:col + LANES] = val.astype(BF16)
                tot = val if tot is None else tot + val
            l_buf[rows, :] = tot if c == 0 else l_buf[rows, :] + tot

    def out_project(b, live):
        row0 = jnp.maximum(b, 0) * BLOCK_ROWS
        prod = jnp.dot(o_buf[...], w_attn[3], preferred_element_type=F32)

        def get(r, col):
            old = h[row0 + r, :, col:col + LANES].astype(F32)
            val = old + (prod[r * width:(r + 1) * width, col:col + LANES] + b_attn[3, 0:1, col:col + LANES])
            return val if live is None else jnp.where(live, val, old)

        def put(r, col, val):
            h[row0 + r, :, col:col + LANES] = val

        finish(get, put, live)

    def score_block(i, before):
        q_val = q[pl.ds(pl.multiple_of(i * blk, blk), blk), :]
        for c in range(n_chunk):
            if c == 2 and before is not None:
                before()
            score_chunk(q_val, c)
        for r in range(BLOCK_ROWS):
            rows = slice(r * width, (r + 1) * width)
            top = jnp.max(m_buf[0, rows, :], axis=1, keepdims=True) * exp_scale
            m_buf[1, rows, :] = jnp.broadcast_to(top, (width, LANES))

    def weigh_block(more):
        for r in range(BLOCK_ROWS):
            rows = slice(r * width, (r + 1) * width)
            inv = 1.0 / jnp.sum(l_buf[rows, :], axis=1, keepdims=True)
            m_buf[2, rows, :] = jnp.broadcast_to(inv, (width, LANES))
        tot = None
        for c in range(n_chunk):
            cols = slice(c * kv_chunk, (c + 1) * kv_chunk)
            part = jnp.dot(p_buf[:, cols], v[cols, :], preferred_element_type=F32)
            tot = part if tot is None else tot + part
            if more:
                prob_chunk(c)
        o_raw[...] = tot

    def scale_o():
        for r in range(BLOCK_ROWS):
            rows = slice(r * width, (r + 1) * width)
            for col in range(0, chan, LANES):
                o_buf[rows, col:col + LANES] = (o_raw[rows, col:col + LANES] * m_buf[2, rows, :]).astype(BF16)

    def attention():
        for copy in attn_copies:
            copy.wait()
        lax.fori_loop(0, n_blk, project, 0)
        zero_stats()
        o_raw[...] = jnp.zeros_like(o_raw)
        m_buf[2] = jnp.zeros((blk, LANES), F32)
        score_block(0, None)

        @pl.when(me >= 0)
        def _():
            for c in range(n_chunk):
                prob_chunk(c)

        def step(i, carry):
            @pl.when(me >= 0)
            def _():
                scale_o()
                score_block(i + 1, lambda: out_project(i - 1, i > 0))

            weigh_block(True)
            return carry

        lax.fori_loop(0, n_blk - 1, step, 0)
        scale_o()
        out_project(n_blk - 2, None)
        weigh_block(False)
        scale_o()
        out_project(n_blk - 1, None)

    def stage(r, carry):
        set_coefs(3 * r, 0.5)
        conv_pass(h, t, 2 * r, False, 0, n_blk // 2)
        set_coefs(3 * r + 1, 0.5)

        @pl.when(r == 1)
        def _():
            for copy in keep:
                copy.start()

        last = r == 1
        conv_pass(t, h, 2 * r + 1, True, jnp.where(last, far_row, 0), jnp.where(last, n_blk // 4, n_blk // 2))

        @pl.when(r == 0)
        def _():
            set_coefs(2, 1.0)
            attention()

        return carry

    keep = [
        pltpu.make_async_copy(t, t_out, sems.at[10]),
        pltpu.make_async_copy(h.at[pl.ds(own_row, half)], h_out, sems.at[11]),
        pltpu.make_async_copy(coef, coef_out, sems.at[12]),
    ]
    lax.fori_loop(0, 2, stage, 0)

    copies = [
        pltpu.make_async_copy(h.at[pl.ds(lax.rem(me + n_dev // 2, n_dev) * band, band)], far_out, sems.at[13]),
        pltpu.make_async_copy(h.at[pl.ds((n_dev - 1 - me) * band, band)], cross_out, sems.at[14]),
    ]
    for copy in copies:
        copy.start()
    for copy in keep + copies:
        copy.wait()


def activate_row(src, row, coef, buf, r, live):
    width, chan = src.shape[1], src.shape[2]
    rows = BLOCK_ROWS + 2
    sub = lax.broadcasted_iota(jnp.int32, (8, LANES), 0)
    for col in range(0, chan, LANES):
        gain = coef[0, 0:1, col:col + LANES]
        shift = coef[1, 0:1, col:col + LANES]
        z = src[row, :, col:col + LANES].astype(F32) * gain + shift
        u = z + z * jnp.tanh(z)
        if live is not None:
            u = jnp.where(live, u, 0.0)
        left = pltpu.roll(u, 1, 0)
        left = jnp.concatenate([jnp.where(sub == 0, 0.0, left[:8]), left[8:]], axis=0)
        right = pltpu.roll(u, width - 1, 0)
        right = jnp.concatenate([right[:-8], jnp.where(sub == 7, 0.0, right[-8:])], axis=0)
        for dx, val in enumerate((left, u, right)):
            first = (dx * rows + r) * width
            buf[first:first + width, col:col + LANES] = val.astype(BF16)


def dots_of(buf, w, acc):
    chan = buf.shape[1]
    rows = BLOCK_ROWS + 2
    width = buf.shape[0] // (3 * rows)
    tot = None
    for dy in range(3):
        for dx in range(3):
            first = (dx * rows + dy) * width
            tap = (3 * dy + dx) * chan
            part = jnp.dot(buf[first:first + BLOCK_ROWS * width, :], w[tap:tap + chan, :], preferred_element_type=F32)
            tot = part if tot is None else tot + part
    acc[...] = tot


def run_sample(sample, me, x, w_in, b_in, w_conv, b_conv, gn_scale, gn_shift, w_attn, w_key, b_attn, b_key, n_dev, n_rows, width):
    chan = w_in.shape[1]
    tokens = n_rows * width
    blk = BLOCK_ROWS * width
    vmem = pl.BlockSpec(memory_space=pltpu.VMEM)
    hbm = pl.BlockSpec(memory_space=pl.ANY)
    flops = 2 * tokens * (7 * 9 * chan * chan // 2 + 4 * chan * chan + 2 * tokens * chan)
    band = jax.ShapeDtypeStruct((n_rows // n_dev, width, chan), BF16)
    return pl.pallas_call(
        functools.partial(sample_kernel, sample),
        out_shape=[
            band,
            band,
            jax.ShapeDtypeStruct((n_rows, width, chan), BF16),
            jax.ShapeDtypeStruct((n_rows // 2, width, chan), BF16),
            jax.ShapeDtypeStruct((2, 8, chan), F32),
        ],
        in_specs=[pl.BlockSpec(memory_space=pltpu.SMEM), hbm, vmem, vmem, hbm, vmem, vmem, vmem, hbm, hbm, vmem, vmem],
        out_specs=[hbm] * 5,
        scratch_shapes=[
            pltpu.VMEM(w_conv.shape, BF16),
            pltpu.VMEM(w_attn.shape, BF16),
            pltpu.VMEM((n_rows, width, chan), BF16),
            pltpu.VMEM((n_rows, width, chan), BF16),
            pltpu.VMEM((chan, tokens), BF16),
            pltpu.VMEM((tokens, chan), BF16),
            pltpu.VMEM((blk, tokens), F32),
            pltpu.VMEM((blk, tokens), BF16),
            pltpu.VMEM((blk, chan), BF16),
            pltpu.VMEM((blk, chan), F32),
            pltpu.VMEM((3, blk, LANES), F32),
            pltpu.VMEM((blk, LANES), F32),
            pltpu.VMEM((4, 8, chan), F32),
            pltpu.VMEM((4, 5, 1, chan), F32),
            pltpu.SemaphoreType.DMA((15,)),
        ],
        compiler_params=pltpu.CompilerParams(vmem_limit_bytes=67_043_328),
        cost_estimate=pl.CostEstimate(flops=flops, bytes_accessed=40 << 20, transcendentals=tokens * tokens),
        name='sample_block',
    )(me, x, w_in, b_in, w_conv, b_conv, gn_scale, gn_shift, w_attn, w_key, b_attn, b_key)


def last_kernel(n_own, n_dev, me_ref, w_hbm, b_ref, *rest):
    kept = [rest[3 * s:3 * s + 3] for s in range(n_own)]
    rest = rest[3 * n_own:]
    n_early = 2 * (n_own - 1)
    early = rest[:n_early]
    out, near_out, w, tb, hb, coefs, buf_a, buf_b, acc, staged, bias, sems = rest[n_early:]
    n_rows, width, chan = kept[0][0].shape
    band = n_rows // n_dev
    span = tb.shape[1]
    n_job = 2 * n_own
    me = me_ref[0]
    near = me + 1 - 2 * lax.rem(me, 2)
    acc_a, acc_b = acc.at[:, 0:chan], acc.at[:, chan:2 * chan]

    def band_of(k):
        return jnp.where(k < n_own, near, me)

    def first_row(k):
        return jnp.clip(band_of(k) * band - 1, 0, n_rows - span)

    w_copy = pltpu.make_async_copy(w_hbm.at[3], w, sems.at[0])
    loads = []
    for k in range(n_job):
        t_hbm, h_hbm, coef_hbm = kept[k % n_own]
        own_row = (me // (n_dev // 2)) * (n_rows // 2)
        loads.append(pltpu.make_async_copy(t_hbm.at[pl.ds(first_row(k), span)], tb.at[k], sems.at[1 + k]))
        loads.append(pltpu.make_async_copy(h_hbm.at[pl.ds(band_of(k) * band - own_row, band)], hb.at[k], sems.at[1 + n_job + k]))
        if k < n_own:
            loads.append(pltpu.make_async_copy(coef_hbm, coefs.at[k], sems.at[1 + 3 * n_job + k]))
    loads[0].start()
    loads[2].start()
    w_copy.start()
    for i, load in enumerate(loads):
        if i not in (0, 2):
            load.start()
    early_in, early_out = [], []
    for i, piece in enumerate(early):
        s, d = divmod(i, 2)
        owner = (n_dev - 1 - me) if d else lax.rem(me + n_dev // 2, n_dev)
        base = 1 + 4 * n_job
        early_in.append(pltpu.make_async_copy(piece, staged.at[i], sems.at[base + i]))
        early_out.append(pltpu.make_async_copy(staged.at[i], out.at[owner * n_own + s], sems.at[base + n_early + i]))
    for copy in early_in:
        copy.start()
    bias[...] = b_ref[3:4, :].astype(F32)

    def store_near(k):
        return pltpu.make_async_copy(hb.at[k], near_out.at[k], sems.at[1 + 2 * n_job + k])

    def store_own(k):
        return pltpu.make_async_copy(hb.at[k], out.at[me * n_own + (k - n_own)], sems.at[1 + 2 * n_job + k])

    def prep(k, b, buf):
        for r in range(BLOCK_ROWS + 2):
            row = band_of(k) * band + (b * BLOCK_ROWS + r - 1)
            row_c = jnp.clip(row, 0, n_rows - 1) - first_row(k)
            live = (row >= 0) & (row < n_rows) if r in (0, BLOCK_ROWS + 1) else None
            activate_row(tb.at[k], row_c, coefs.at[lax.rem(k, n_own)], buf, r, live)

    def finish(k, b, part, live):
        k = jnp.maximum(k, 0)
        for col in range(0, chan, LANES):
            for r in range(BLOCK_ROWS):
                row = b * BLOCK_ROWS + r
                old = hb[k, row, :, col:col + LANES].astype(F32)
                val = old + (part[r * width:(r + 1) * width, col:col + LANES] + bias[0:1, col:col + LANES])
                if live is not None:
                    val = jnp.where(live, val, old)
                hb[k, row, :, col:col + LANES] = val.astype(BF16)

    loads[0].wait()
    loads[2].wait()
    prep(jnp.int32(0), 0, buf_a)
    w_copy.wait()
    for i, load in enumerate(loads):
        if i not in (0, 2):
            load.wait()

    def job(k, carry):
        @pl.when((k >= 2) & (k < n_own + 2))
        def _():
            store_near(k - 2).start()

        @pl.when(k >= n_own + 2)
        def _():
            store_own(k - 2).start()

        @pl.when(k == 2)
        def _():
            for load, store in zip(early_in, early_out):
                load.wait()
                store.start()

        dots_of(buf_a, w, acc_a)
        prep(k, 1, buf_b)
        finish(k - 1, 1, acc_b, k > 0)
        dots_of(buf_b, w, acc_b)
        prep(jnp.minimum(k + 1, n_job - 1), 0, buf_a)
        finish(k, 0, acc_a, None)
        return carry

    lax.fori_loop(0, n_job, job, 0)
    finish(jnp.int32(n_job - 1), 1, acc_b, None)
    store_own(n_job - 2).start()
    store_own(n_job - 1).start()
    for store in early_out:
        store.wait()
    for k in range(n_job):
        (store_near if k < n_own else store_own)(k).wait()


def run_last(me, w_conv, b_conv, kept, early, n_dev, out_shape):
    n_own = len(kept)
    n_rows, width, chan = kept[0][0].shape
    band = n_rows // n_dev
    blk = BLOCK_ROWS * width
    n_job = 2 * n_own
    vmem = pl.BlockSpec(memory_space=pltpu.VMEM)
    hbm = pl.BlockSpec(memory_space=pl.ANY)
    args = [ref for refs in kept for ref in refs] + list(early)
    return pl.pallas_call(
        functools.partial(last_kernel, n_own, n_dev),
        out_shape=[jax.ShapeDtypeStruct(out_shape, BF16), jax.ShapeDtypeStruct((n_own, band, width, chan), BF16)],
        in_specs=[pl.BlockSpec(memory_space=pltpu.SMEM), hbm, vmem] + [hbm] * len(args),
        out_specs=[hbm, hbm],
        scratch_shapes=[
            pltpu.VMEM(w_conv.shape[1:], BF16),
            pltpu.VMEM((n_job, band + 2, width, chan), BF16),
            pltpu.VMEM((n_job, band, width, chan), BF16),
            pltpu.VMEM((n_own, 2, 8, chan), F32),
            pltpu.VMEM((3 * (BLOCK_ROWS + 2) * width, chan), BF16),
            pltpu.VMEM((3 * (BLOCK_ROWS + 2) * width, chan), BF16),
            pltpu.VMEM((blk, 2 * chan), F32),
            pltpu.VMEM((len(early), band, width, chan), BF16),
            pltpu.VMEM((1, chan), F32),
            pltpu.SemaphoreType.DMA((1 + 4 * n_job + 2 * len(early),)),
        ],
        compiler_params=pltpu.CompilerParams(vmem_limit_bytes=67_043_328),
        cost_estimate=pl.CostEstimate(flops=2 * n_job * band * width * 9 * chan * chan, bytes_accessed=40 << 20, transcendentals=0),
        name='last_conv',
    )(me, w_conv, b_conv, *args)


def place_kernel(n_own, n_dev, me_ref, near_ref, far_ref, cross_ref, base_ref, out, stage, in_sems, out_sems):
    del base_ref
    me = me_ref[0]
    near = me + 1 - 2 * lax.rem(me, 2)
    moves = [(near_ref.at[s], near * n_own + s) for s in range(n_own)]
    moves.append((far_ref, lax.rem(me + n_dev // 2, n_dev) * n_own + (n_own - 1)))
    moves.append((cross_ref, (n_dev - 1 - me) * n_own + (n_own - 1)))
    loads = [pltpu.make_async_copy(src, stage.at[i], in_sems.at[i]) for i, (src, _) in enumerate(moves)]
    stores = [pltpu.make_async_copy(stage.at[i], out.at[at], out_sems.at[i]) for i, (_, at) in enumerate(moves)]
    for load in loads:
        load.start()
    for load, store in zip(loads, stores):
        load.wait()
        store.start()
    for store in stores:
        store.wait()


def place(me, near, far, cross, base, n_dev):
    n_own = near.shape[0]
    hbm = pl.BlockSpec(memory_space=pl.ANY)
    n_move = n_own + 2
    return pl.pallas_call(
        functools.partial(place_kernel, n_own, n_dev),
        out_shape=jax.ShapeDtypeStruct(base.shape, BF16),
        in_specs=[pl.BlockSpec(memory_space=pltpu.SMEM)] + [hbm] * 4,
        out_specs=hbm,
        input_output_aliases={4: 0},
        scratch_shapes=[
            pltpu.VMEM((n_move,) + tuple(far.shape), BF16),
            pltpu.SemaphoreType.DMA((n_move,)),
            pltpu.SemaphoreType.DMA((n_move,)),
        ],
        cost_estimate=pl.CostEstimate(flops=1 << 20, bytes_accessed=n_move << 21, transcendentals=0),
        name='place_bands',
    )(me, near, far, cross, base)


def solution(mesh):
    n_dev = mesh.shape['cp']

    def local_fn(latents, w_in, b_in, w_conv, b_conv, gn_scale, gn_shift, w_attn, b_attn):
        me = lax.axis_index('cp').astype(jnp.int32).reshape(1)
        lat = lax.all_to_all(latents, 'cp', split_axis=0, concat_axis=1, tiled=True)
        n_own, n_rows, width, n_lat = lat.shape
        chan = w_in.shape[-1]
        tokens = n_rows * width
        flat = jnp.transpose(lat.reshape(n_own, tokens, n_lat), (0, 2, 1))
        flat = jnp.pad(flat, ((0, 0), (0, 0), (width + 1, width + 1)))
        col_pos = lax.broadcasted_iota(jnp.int32, (1, 1, tokens), 2) % width
        taps = []
        for dy in range(3):
            for dx in range(3):
                tap = flat[:, :, dy * width + dx:dy * width + dx + tokens]
                if dx == 0:
                    tap = jnp.where(col_pos == 0, jnp.zeros_like(tap), tap)
                if dx == 2:
                    tap = jnp.where(col_pos == width - 1, jnp.zeros_like(tap), tap)
                taps.append(tap)
        cols = jnp.concatenate(taps, axis=1)
        w_in2 = w_in.reshape(9 * n_lat, chan)
        w_conv2 = w_conv.reshape(4, 9 * chan, chan)
        w_key = w_attn[1].T
        b_key = b_attn[1].astype(F32).reshape(chan, 1)
        b_in2 = b_in.astype(F32).reshape(1, chan)
        out_shape = (n_own * n_dev, n_rows // n_dev, width, chan)
        kept, moved = [], []
        for s in range(n_own):
            far, cross, *keep = run_sample(s, me, cols, w_in2, b_in2, w_conv2, b_conv, gn_scale, gn_shift, w_attn, w_key,
                                           b_attn, b_key, n_dev, n_rows, width)
            kept.append(keep)
            moved.append(lax.ppermute(far, 'cp', [(j, (j + n_dev // 2) % n_dev) for j in range(n_dev)]))
            moved.append(lax.ppermute(cross, 'cp', [(j, n_dev - 1 - j) for j in range(n_dev)]))
        out, near = run_last(me, w_conv2, b_conv, kept, moved[:-2], n_dev, out_shape)
        near = lax.ppermute(near, 'cp', [(j, j ^ 1) for j in range(n_dev)])
        return place(me, near, moved[-2], moved[-1], out, n_dev)

    band_spec = P('dp', 'cp')
    whole_spec = P()
    return jax.shard_map(local_fn, mesh=mesh, in_specs=(band_spec,) + (whole_spec,) * 8, out_specs=band_spec, check_vma=False)
```

profile of v0, /device:TPU:1, one launch (start us, length us, event | category | flops | bytes accessed | tf_op | source)
XLA Modules:
  0.0 743.7 jit_solution(7519732109663672878)
XLA Ops:
  0.0 2.6 reshape.60
  2.6 4.3 all-to-all-start
  6.8 1.3 reshape.57
  8.1 0.7 bitcast_convert_fusion
  8.8 0.9 copy.15.b_key_ref
  9.6 1.1 slice.39
  10.7 1.0 copy.19
  11.7 2.8 all-to-all-done
  14.5 0.7 reshape.61
  15.2 0.3 copy.21
  15.5 0.8 reshape.53
  16.3 0.2 select_dynamic-update-slice_fusion.5
  16.8 0.2 select_dynamic-update-slice_fusion.4
  17.0 0.2 select_dynamic-update-slice_fusion.3
  17.3 0.2 select_dynamic-update-slice_fusion.2
  17.5 0.2 select_dynamic-update-slice_fusion.1
  18.2 2.2 copy-done.2
  20.4 141.3 %sample_block.6 = (bf16[16,64,512]{2,1,0:T(8,128)(2,1)}, bf16[16,64,512]{2,1,0:T(8,128)(2,1)}, bf16[64,64,512]{2,1,0:T(8,128)(2,1)}, bf16[32,64,512]{2,1,0:T(8,128)(2,1)}, f32[2,8,512]{2,1,0:T(8,128)}) custom-call(s32[1]{0:T(128)} %bitcast.me_ref, bf16[4,144,4096]{2,1,0:T(8,128)(2,1)} %copy-done.2, bf16[144,512]{1,0:T(8,128)(2,1)} %bitcast.46, ...), custom_call_target="tpu_custom_call" | custom-call | flops 110595407872 | bytes 41943040 | tf_op jit(solution)/shard_map/sample_block/pallas_call | solution.py:347
  161.6 156.0 %sample_block.5 = (bf16[16,64,512]{2,1,0:T(8,128)(2,1)}, bf16[16,64,512]{2,1,0:T(8,128)(2,1)}, bf16[64,64,512]{2,1,0:T(8,128)(2,1)}, bf16[32,64,512]{2,1,0:T(8,128)(2,1)}, f32[2,8,512]{2,1,0:T(8,128)}) custom-call(s32[1]{0:T(128)} %bitcast.me_ref, bf16[4,144,4096]{2,1,0:T(8,128)(2,1)} %copy-done.2, bf16[144,512]{1,0:T(8,128)(2,1)} %bitcast.47, ...), custom_call_target="tpu_custom_call" | custom-call | flops 110595407872 | bytes 41943040 | tf_op jit(solution)/shard_map/sample_block/pallas_call | solution.py:347
  317.7 0.7 collective-permute-start.4
  318.3 156.1 %sample_block.4 = (bf16[16,64,512]{2,1,0:T(8,128)(2,1)}, bf16[16,64,512]{2,1,0:T(8,128)(2,1)}, bf16[64,64,512]{2,1,0:T(8,128)(2,1)}, bf16[32,64,512]{2,1,0:T(8,128)(2,1)}, f32[2,8,512]{2,1,0:T(8,128)}) custom-call(s32[1]{0:T(128)} %bitcast.me_ref, bf16[4,144,4096]{2,1,0:T(8,128)(2,1)} %copy-done.2, bf16[144,512]{1,0:T(8,128)(2,1)} %bitcast.48, ...), custom_call_target="tpu_custom_call" | custom-call | flops 110595407872 | bytes 41943040 | tf_op jit(solution)/shard_map/sample_block/pallas_call | solution.py:347
  474.4 2.1 collective-permute-start.5
  476.6 0.6 collective-permute-start.3
  477.3 1.0 collective-permute-start
  478.3 1.7 collective-permute-start.1
  480.0 155.9 %sample_block.7 = (bf16[16,64,512]{2,1,0:T(8,128)(2,1)}, bf16[16,64,512]{2,1,0:T(8,128)(2,1)}, bf16[64,64,512]{2,1,0:T(8,128)(2,1)}, bf16[32,64,512]{2,1,0:T(8,128)(2,1)}, f32[2,8,512]{2,1,0:T(8,128)}) custom-call(s32[1]{0:T(128)} %bitcast.me_ref, bf16[4,144,4096]{2,1,0:T(8,128)(2,1)} %copy-done.2, bf16[144,512]{1,0:T(8,128)(2,1)} %bitcast.49, ...), custom_call_target="tpu_custom_call" | custom-call | flops 110595407872 | bytes 41943040 | tf_op jit(solution)/shard_map/sample_block/pallas_call | solution.py:347
  636.0 53.4 %last_conv.1 = (bf16[16,16,64,512]{3,2,1,0:T(8,128)(2,1)}, bf16[4,16,64,512]{3,2,1,0:T(8,128)(2,1)}) custom-call(s32[1]{0:T(128)} %bitcast.me_ref, bf16[4,4608,512]{2,1,0:T(8,128)(2,1)} %bitcast.45, bf16[4,512]{1,0:T(4,128)(2,1)} %b_ref.1, bf16[64,64,512]{2,1,0:T(8,128)(2,1)} %get-tuple-element.27.rest_0_, bf16[32,64,512]{2,1,0:T(8,128)(2,1)} %get-tuple-element.28.rest_1_, ...), custom_call_target="tpu_custom_call" | custom-call | flops 38654705664 | bytes 41943040 | tf_op jit(solution)/shard_map/last_conv/pallas_call | solution.py:501
  689.6 2.0 collective-permute-start.8
  691.5 22.3 %collective-permute-done.7.far_ref = bf16[16,64,512]{2,1,0:T(8,128)(2,1)S(1)} collective-permute-done((bf16[16,64,512]{2,1,0:T(8,128)(2,1)}, bf16[16,64,512]{2,1,0:T(8,128)(2,1)S(1)}, u32[]{:S(2)}, u32[]{:S(2)}) %collective-permute-start.7) | collective-permute-done | bytes 1048608 | tf_op jit(solution)/shard_map/ppermute | solution.py:595
  713.9 23.1 %collective-permute-done.8.cross_ref = bf16[16,64,512]{2,1,0:T(8,128)(2,1)S(1)} collective-permute-done((bf16[16,64,512]{2,1,0:T(8,128)(2,1)}, bf16[16,64,512]{2,1,0:T(8,128)(2,1)S(1)}, u32[]{:S(2)}, u32[]{:S(2)}) %collective-permute-start.8) | collective-permute-done | bytes 1048608 | tf_op jit(solution)/shard_map/ppermute | solution.py:596
  737.0 1.0 copy-done.1
  738.0 5.5 place_bands.1
  (20 shorter events, 1.0 us)
Async XLA Ops:
  2.6 11.9 %all-to-all-start = ((bf16[4,2,32768]{2,1,0:T(2,128)(2,1)}), bf16[4,2,32768]{2,1,0:T(2,128)(2,1)S(1)}, u32[]{:S(2)}, u32[]{:S(2)}) async-start(bf16[4,2,32768]{2,1,0:T(2,128)(2,1)} %reshape.60), calls=%async_computation | async-start | bytes 1048576 | tf_op jit(solution)/shard_map/all_to_all | solution.py:567
  18.2 2.2 copy-start.2
  317.7 160.7 %collective-permute-start.4 = (bf16[16,64,512]{2,1,0:T(8,128)(2,1)}, bf16[16,64,512]{2,1,0:T(8,128)(2,1)}, u32[]{:S(2)}, u32[]{:S(2)}) collective-permute-start(bf16[16,64,512]{2,1,0:T(8,128)(2,1)} %get-tuple-element.43), channel_id=1, source_target_pairs={{0,2},{1,3},{2,0},{3,1},{4,6},{5,7},{6,4},{7,5}} | collective-permute-start | bytes 3145736 | tf_op jit(solution)/shard_map/ppermute | solution.py:595
  474.4 161.5 %collective-permute-start.5 = (bf16[16,64,512]{2,1,0:T(8,128)(2,1)}, bf16[16,64,512]{2,1,0:T(8,128)(2,1)}, u32[]{:S(2)}, u32[]{:S(2)}) collective-permute-start(bf16[16,64,512]{2,1,0:T(8,128)(2,1)} %get-tuple-element.44), channel_id=1, source_target_pairs={{0,3},{1,2},{2,1},{3,0},{4,7},{5,6},{6,5},{7,4}} | collective-permute-start | bytes 3145736 | tf_op jit(solution)/shard_map/ppermute | solution.py:596
  476.5 159.4 %collective-permute-start.2 = (bf16[16,64,512]{2,1,0:T(8,128)(2,1)}, bf16[16,64,512]{2,1,0:T(8,128)(2,1)}, u32[]{:S(2)}, u32[]{:S(2)}) collective-permute-start(bf16[16,64,512]{2,1,0:T(8,128)(2,1)} %get-tuple-element.41), channel_id=1, source_target_pairs={{0,2},{1,3},{2,0},{3,1},{4,6},{5,7},{6,4},{7,5}} | collective-permute-start | bytes 3145736 | tf_op jit(solution)/shard_map/ppermute | solution.py:595
  476.6 159.3 %collective-permute-start.3 = (bf16[16,64,512]{2,1,0:T(8,128)(2,1)}, bf16[16,64,512]{2,1,0:T(8,128)(2,1)}, u32[]{:S(2)}, u32[]{:S(2)}) collective-permute-start(bf16[16,64,512]{2,1,0:T(8,128)(2,1)} %get-tuple-element.42), channel_id=1, source_target_pairs={{0,3},{1,2},{2,1},{3,0},{4,7},{5,6},{6,5},{7,4}} | collective-permute-start | bytes 3145736 | tf_op jit(solution)/shard_map/ppermute | solution.py:596
  477.3 158.7 %collective-permute-start = (bf16[16,64,512]{2,1,0:T(8,128)(2,1)}, bf16[16,64,512]{2,1,0:T(8,128)(2,1)}, u32[]{:S(2)}, u32[]{:S(2)}) collective-permute-start(bf16[16,64,512]{2,1,0:T(8,128)(2,1)} %get-tuple-element.39), channel_id=1, source_target_pairs={{0,2},{1,3},{2,0},{3,1},{4,6},{5,7},{6,4},{7,5}} | collective-permute-start | bytes 3145736 | tf_op jit(solution)/shard_map/ppermute | solution.py:595
  478.3 157.6 %collective-permute-start.1 = (bf16[16,64,512]{2,1,0:T(8,128)(2,1)}, bf16[16,64,512]{2,1,0:T(8,128)(2,1)}, u32[]{:S(2)}, u32[]{:S(2)}) collective-permute-start(bf16[16,64,512]{2,1,0:T(8,128)(2,1)} %get-tuple-element.40), channel_id=1, source_target_pairs={{0,3},{1,2},{2,1},{3,0},{4,7},{5,6},{6,5},{7,4}} | collective-permute-start | bytes 3145736 | tf_op jit(solution)/shard_map/ppermute | solution.py:596
  689.4 47.6 %collective-permute-start.6 = (bf16[4,16,64,512]{3,2,1,0:T(8,128)(2,1)}, bf16[4,16,64,512]{3,2,1,0:T(8,128)(2,1)}, u32[]{:S(2)}, u32[]{:S(2)}) collective-permute-start(bf16[4,16,64,512]{3,2,1,0:T(8,128)(2,1)} %get-tuple-element.45), channel_id=1, source_target_pairs={{0,1},{1,0},{2,3},{3,2},{4,5},{5,4},{6,7},{7,6}} | collective-permute-start | bytes 12582920 | tf_op jit(solution)/shard_map/ppermute | solution.py:598
  689.4 24.5 %collective-permute-start.7 = (bf16[16,64,512]{2,1,0:T(8,128)(2,1)}, bf16[16,64,512]{2,1,0:T(8,128)(2,1)S(1)}, u32[]{:S(2)}, u32[]{:S(2)}) collective-permute-start(bf16[16,64,512]{2,1,0:T(8,128)(2,1)} %get-tuple-element.46), channel_id=1, source_target_pairs={{0,2},{1,3},{2,0},{3,1},{4,6},{5,7},{6,4},{7,5}} | collective-permute-start | bytes 3145736 | tf_op jit(solution)/shard_map/ppermute | solution.py:595
  689.6 47.5 %collective-permute-start.8 = (bf16[16,64,512]{2,1,0:T(8,128)(2,1)}, bf16[16,64,512]{2,1,0:T(8,128)(2,1)S(1)}, u32[]{:S(2)}, u32[]{:S(2)}) collective-permute-start(bf16[16,64,512]{2,1,0:T(8,128)(2,1)} %get-tuple-element.47), channel_id=1, source_target_pairs={{0,3},{1,2},{2,1},{3,0},{4,7},{5,6},{6,5},{7,4}} | collective-permute-start | bytes 3145736 | tf_op jit(solution)/shard_map/ppermute | solution.py:596
  713.9 23.1 %copy-start = (bf16[16,64,512]{2,1,0:T(8,128)(2,1)}, bf16[16,64,512]{2,1,0:T(8,128)(2,1)S(1)}, u32[]{:S(2)}) copy-start(bf16[16,64,512]{2,1,0:T(8,128)(2,1)S(1)} %collective-permute-done.7.far_ref) | copy-start | bytes 3145732
  737.0 1.0 copy-start.1
where the time goes:
time: 748 us; the launch traced here: 744 us
  Pallas kernels  668 us (89%)
  waiting for transfers between devices  48.2 us (6%)
  starting transfers between devices  12.7 us (2%)
  local copies, waits for them, and re-layouts  10.9 us (1%)
    pallas_call x4, Pallas kernels, run_sample(): pl.pallas_call(functools.partial(sample_kernel, sample), out_shape=[band,...  609 us
    pallas_call x1, Pallas kernels, run_last(): pl.pallas_call(functools.partial(last_kernel, n_own, n_dev), out_shape=[j...  53.4 us
    ppermute x4, waiting for transfers between devices, local_fn(): lax.ppermute(cross, 'cp', [(j, n_dev - 1 - j) for j in range(n_dev)])  23.1 us
    ppermute x4, waiting for transfers between devices, local_fn(): lax.ppermute(far, 'cp', [(j, (j + n_dev // 2) % n_dev) for j in range(n_d...  22.4 us
  transfers between devices with their start and end apart: 10, of which 3 were waited for; matrix products, arithmetic and copies ran while one was open for 1% of the time, Pallas kernels for 42%

commit v1 on v0

--- a/solution.py
+++ b/solution.py
@@ -49,11 +49,6 @@
     x_copy = pltpu.make_async_copy(x_hbm.at[sample], p_buf.at[0:n_cols, :], sems.at[5])
     x_copy.start()
     conv_copy(0).start()
-    conv_copy(1).start()
-    for copy in attn_copies:
-        copy.start()
-    conv_copy(2).start()
-    conv_copy(3).start()
 
     def zero_stats():
         stat[...] = jnp.zeros((2, 8, chan), F32)
@@ -141,6 +136,11 @@
         zero_stats()
         prep(src, buf_a, 0, base)
         conv_copy(idx).wait()
+        if not residual:
+            @pl.when(idx == 0)
+            def _():
+                for copy in [conv_copy(1)] + attn_copies + [conv_copy(2), conv_copy(3)]:
+                    copy.start()
 
         def pair(j, carry):
             conv_dots(buf_a, acc_a, idx)
@@ -407,12 +407,10 @@
         loads.append(pltpu.make_async_copy(h_hbm.at[pl.ds(band_of(k) * band - own_row, band)], hb.at[k], sems.at[1 + n_job + k]))
         if k < n_own:
             loads.append(pltpu.make_async_copy(coef_hbm, coefs.at[k], sems.at[1 + 3 * n_job + k]))
-    loads[0].start()
-    loads[2].start()
+    first_loads, later_loads = loads[:6], loads[6:]
     w_copy.start()
-    for i, load in enumerate(loads):
-        if i not in (0, 2):
-            load.start()
+    for load in first_loads:
+        load.start()
     early_in, early_out = [], []
     for i, piece in enumerate(early):
         s, d = divmod(i, 2)
@@ -420,8 +418,6 @@
         base = 1 + 4 * n_job
         early_in.append(pltpu.make_async_copy(piece, staged.at[i], sems.at[base + i]))
         early_out.append(pltpu.make_async_copy(staged.at[i], out.at[owner * n_own + s], sems.at[base + n_early + i]))
-    for copy in early_in:
-        copy.start()
     bias[...] = b_ref[3:4, :].astype(F32)
 
     def store_near(k):
@@ -448,13 +444,12 @@
                     val = jnp.where(live, val, old)
                 hb[k, row, :, col:col + LANES] = val.astype(BF16)
 
-    loads[0].wait()
-    loads[2].wait()
+    for load in first_loads:
+        load.wait()
     prep(jnp.int32(0), 0, buf_a)
     w_copy.wait()
-    for i, load in enumerate(loads):
-        if i not in (0, 2):
-            load.wait()
+    for load in later_loads:
+        load.start()
 
     def job(k, carry):
         @pl.when((k >= 2) & (k < n_own + 2))
@@ -465,7 +460,14 @@
         def _():
             store_own(k - 2).start()
 
-        @pl.when(k == 2)
+        @pl.when(k == 1)
+        def _():
+            for load in later_loads:
+                load.wait()
+            for load in early_in:
+                load.start()
+
+        @pl.when(k == 3)
         def _():
             for load, store in zip(early_in, early_out):
                 load.wait()

time: 748 us -> 745 us (level)
  no operation moved by 1% of the time
where the time goes in v1:
time: 745 us; the launch traced here: 741 us
  Pallas kernels  665 us (89%)
  waiting for transfers between devices  48.2 us (6%)
  starting transfers between devices  12.7 us (2%)
  local copies, waits for them, and re-layouts  10.9 us (1%)
    pallas_call x4, Pallas kernels, run_sample(): pl.pallas_call(functools.partial(sample_kernel, sample), out_shape=[band,...  609 us
    pallas_call x1, Pallas kernels, run_last(): pl.pallas_call(functools.partial(last_kernel, n_own, n_dev), out_shape=[j...  50.6 us
    ppermute x4, waiting for transfers between devices, local_fn(): lax.ppermute(cross, 'cp', [(j, n_dev - 1 - j) for j in range(n_dev)])  23.1 us
    ppermute x4, waiting for transfers between devices, local_fn(): lax.ppermute(far, 'cp', [(j, (j + n_dev // 2) % n_dev) for j in range(n_d...  22.4 us
  transfers between devices with their start and end apart: 10, of which 3 were waited for; matrix products, arithmetic and copies ran while one was open for 1% of the time, Pallas kernels for 42%

profile of v1, /device:TPU:1, one launch (start us, length us, event | category | flops | bytes accessed | tf_op | source)
XLA Modules:
  0.0 740.9 jit_solution(17671682044438519227)
XLA Ops:
  0.0 2.6 reshape.60
  2.6 4.3 all-to-all-start
  6.8 1.3 reshape.57
  8.1 0.7 bitcast_convert_fusion
  8.8 0.9 copy.15.b_key_ref
  9.6 1.1 slice.39
  10.7 1.0 copy.19
  11.7 2.8 all-to-all-done
  14.5 0.7 reshape.61
  15.2 0.3 copy.21
  15.5 0.8 reshape.53
  16.3 0.2 select_dynamic-update-slice_fusion.5
  16.8 0.2 select_dynamic-update-slice_fusion.4
  17.0 0.2 select_dynamic-update-slice_fusion.3
  17.3 0.2 select_dynamic-update-slice_fusion.2
  17.5 0.2 select_dynamic-update-slice_fusion.1
  18.2 2.2 copy-done.2
  20.4 141.3 %sample_block.6 = (bf16[16,64,512]{2,1,0:T(8,128)(2,1)}, bf16[16,64,512]{2,1,0:T(8,128)(2,1)}, bf16[64,64,512]{2,1,0:T(8,128)(2,1)}, bf16[32,64,512]{2,1,0:T(8,128)(2,1)}, f32[2,8,512]{2,1,0:T(8,128)}) custom-call(s32[1]{0:T(128)} %bitcast.me_ref, bf16[4,144,4096]{2,1,0:T(8,128)(2,1)} %copy-done.2, bf16[144,512]{1,0:T(8,128)(2,1)} %bitcast.46, ...), custom_call_target="tpu_custom_call" | custom-call | flops 110595407872 | bytes 41943040 | tf_op jit(solution)/shard_map/sample_block/pallas_call | solution.py:347
  161.6 156.0 %sample_block.5 = (bf16[16,64,512]{2,1,0:T(8,128)(2,1)}, bf16[16,64,512]{2,1,0:T(8,128)(2,1)}, bf16[64,64,512]{2,1,0:T(8,128)(2,1)}, bf16[32,64,512]{2,1,0:T(8,128)(2,1)}, f32[2,8,512]{2,1,0:T(8,128)}) custom-call(s32[1]{0:T(128)} %bitcast.me_ref, bf16[4,144,4096]{2,1,0:T(8,128)(2,1)} %copy-done.2, bf16[144,512]{1,0:T(8,128)(2,1)} %bitcast.47, ...), custom_call_target="tpu_custom_call" | custom-call | flops 110595407872 | bytes 41943040 | tf_op jit(solution)/shard_map/sample_block/pallas_call | solution.py:347
  317.7 0.7 collective-permute-start.4
  318.4 156.1 %sample_block.4 = (bf16[16,64,512]{2,1,0:T(8,128)(2,1)}, bf16[16,64,512]{2,1,0:T(8,128)(2,1)}, bf16[64,64,512]{2,1,0:T(8,128)(2,1)}, bf16[32,64,512]{2,1,0:T(8,128)(2,1)}, f32[2,8,512]{2,1,0:T(8,128)}) custom-call(s32[1]{0:T(128)} %bitcast.me_ref, bf16[4,144,4096]{2,1,0:T(8,128)(2,1)} %copy-done.2, bf16[144,512]{1,0:T(8,128)(2,1)} %bitcast.48, ...), custom_call_target="tpu_custom_call" | custom-call | flops 110595407872 | bytes 41943040 | tf_op jit(solution)/shard_map/sample_block/pallas_call | solution.py:347
  474.5 2.1 collective-permute-start.5
  476.7 0.6 collective-permute-start.3
  477.3 1.1 collective-permute-start
  478.3 1.7 collective-permute-start.1
  480.1 155.9 %sample_block.7 = (bf16[16,64,512]{2,1,0:T(8,128)(2,1)}, bf16[16,64,512]{2,1,0:T(8,128)(2,1)}, bf16[64,64,512]{2,1,0:T(8,128)(2,1)}, bf16[32,64,512]{2,1,0:T(8,128)(2,1)}, f32[2,8,512]{2,1,0:T(8,128)}) custom-call(s32[1]{0:T(128)} %bitcast.me_ref, bf16[4,144,4096]{2,1,0:T(8,128)(2,1)} %copy-done.2, bf16[144,512]{1,0:T(8,128)(2,1)} %bitcast.49, ...), custom_call_target="tpu_custom_call" | custom-call | flops 110595407872 | bytes 41943040 | tf_op jit(solution)/shard_map/sample_block/pallas_call | solution.py:347
  636.0 50.6 %last_conv.1 = (bf16[16,16,64,512]{3,2,1,0:T(8,128)(2,1)}, bf16[4,16,64,512]{3,2,1,0:T(8,128)(2,1)}) custom-call(s32[1]{0:T(128)} %bitcast.me_ref, bf16[4,4608,512]{2,1,0:T(8,128)(2,1)} %bitcast.45, bf16[4,512]{1,0:T(4,128)(2,1)} %b_ref.1, bf16[64,64,512]{2,1,0:T(8,128)(2,1)} %get-tuple-element.27.rest_0_, bf16[32,64,512]{2,1,0:T(8,128)(2,1)} %get-tuple-element.28.rest_1_, ...), custom_call_target="tpu_custom_call" | custom-call | flops 38654705664 | bytes 41943040 | tf_op jit(solution)/shard_map/last_conv/pallas_call | solution.py:503
  686.6 2.1 collective-permute-start.8
  688.7 22.3 %collective-permute-done.7.far_ref = bf16[16,64,512]{2,1,0:T(8,128)(2,1)S(1)} collective-permute-done((bf16[16,64,512]{2,1,0:T(8,128)(2,1)}, bf16[16,64,512]{2,1,0:T(8,128)(2,1)S(1)}, u32[]{:S(2)}, u32[]{:S(2)}) %collective-permute-start.7) | collective-permute-done | bytes 1048608 | tf_op jit(solution)/shard_map/ppermute | solution.py:597
  711.1 23.1 %collective-permute-done.8.cross_ref = bf16[16,64,512]{2,1,0:T(8,128)(2,1)S(1)} collective-permute-done((bf16[16,64,512]{2,1,0:T(8,128)(2,1)}, bf16[16,64,512]{2,1,0:T(8,128)(2,1)S(1)}, u32[]{:S(2)}, u32[]{:S(2)}) %collective-permute-start.8) | collective-permute-done | bytes 1048608 | tf_op jit(solution)/shard_map/ppermute | solution.py:598
  734.2 1.0 copy-done.1
  735.1 5.5 place_bands.1
  (20 shorter events, 0.9 us)
Async XLA Ops:
  2.6 11.9 %all-to-all-start = ((bf16[4,2,32768]{2,1,0:T(2,128)(2,1)}), bf16[4,2,32768]{2,1,0:T(2,128)(2,1)S(1)}, u32[]{:S(2)}, u32[]{:S(2)}) async-start(bf16[4,2,32768]{2,1,0:T(2,128)(2,1)} %reshape.60), calls=%async_computation | async-start | bytes 1048576 | tf_op jit(solution)/shard_map/all_to_all | solution.py:569
  18.2 2.2 copy-start.2
  317.7 160.7 %collective-permute-start.4 = (bf16[16,64,512]{2,1,0:T(8,128)(2,1)}, bf16[16,64,512]{2,1,0:T(8,128)(2,1)}, u32[]{:S(2)}, u32[]{:S(2)}) collective-permute-start(bf16[16,64,512]{2,1,0:T(8,128)(2,1)} %get-tuple-element.43), channel_id=1, source_target_pairs={{0,2},{1,3},{2,0},{3,1},{4,6},{5,7},{6,4},{7,5}} | collective-permute-start | bytes 3145736 | tf_op jit(solution)/shard_map/ppermute | solution.py:597
  474.5 161.5 %collective-permute-start.5 = (bf16[16,64,512]{2,1,0:T(8,128)(2,1)}, bf16[16,64,512]{2,1,0:T(8,128)(2,1)}, u32[]{:S(2)}, u32[]{:S(2)}) collective-permute-start(bf16[16,64,512]{2,1,0:T(8,128)(2,1)} %get-tuple-element.44), channel_id=1, source_target_pairs={{0,3},{1,2},{2,1},{3,0},{4,7},{5,6},{6,5},{7,4}} | collective-permute-start | bytes 3145736 | tf_op jit(solution)/shard_map/ppermute | solution.py:598
  476.6 159.4 %collective-permute-start.2 = (bf16[16,64,512]{2,1,0:T(8,128)(2,1)}, bf16[16,64,512]{2,1,0:T(8,128)(2,1)}, u32[]{:S(2)}, u32[]{:S(2)}) collective-permute-start(bf16[16,64,512]{2,1,0:T(8,128)(2,1)} %get-tuple-element.41), channel_id=1, source_target_pairs={{0,2},{1,3},{2,0},{3,1},{4,6},{5,7},{6,4},{7,5}} | collective-permute-start | bytes 3145736 | tf_op jit(solution)/shard_map/ppermute | solution.py:597
  476.7 159.3 %collective-permute-start.3 = (bf16[16,64,512]{2,1,0:T(8,128)(2,1)}, bf16[16,64,512]{2,1,0:T(8,128)(2,1)}, u32[]{:S(2)}, u32[]{:S(2)}) collective-permute-start(bf16[16,64,512]{2,1,0:T(8,128)(2,1)} %get-tuple-element.42), channel_id=1, source_target_pairs={{0,3},{1,2},{2,1},{3,0},{4,7},{5,6},{6,5},{7,4}} | collective-permute-start | bytes 3145736 | tf_op jit(solution)/shard_map/ppermute | solution.py:598
  477.3 158.7 %collective-permute-start = (bf16[16,64,512]{2,1,0:T(8,128)(2,1)}, bf16[16,64,512]{2,1,0:T(8,128)(2,1)}, u32[]{:S(2)}, u32[]{:S(2)}) collective-permute-start(bf16[16,64,512]{2,1,0:T(8,128)(2,1)} %get-tuple-element.39), channel_id=1, source_target_pairs={{0,2},{1,3},{2,0},{3,1},{4,6},{5,7},{6,4},{7,5}} | collective-permute-start | bytes 3145736 | tf_op jit(solution)/shard_map/ppermute | solution.py:597
  478.3 157.6 %collective-permute-start.1 = (bf16[16,64,512]{2,1,0:T(8,128)(2,1)}, bf16[16,64,512]{2,1,0:T(8,128)(2,1)}, u32[]{:S(2)}, u32[]{:S(2)}) collective-permute-start(bf16[16,64,512]{2,1,0:T(8,128)(2,1)} %get-tuple-element.40), channel_id=1, source_target_pairs={{0,3},{1,2},{2,1},{3,0},{4,7},{5,6},{6,5},{7,4}} | collective-permute-start | bytes 3145736 | tf_op jit(solution)/shard_map/ppermute | solution.py:598
  686.5 47.6 %collective-permute-start.6 = (bf16[4,16,64,512]{3,2,1,0:T(8,128)(2,1)}, bf16[4,16,64,512]{3,2,1,0:T(8,128)(2,1)}, u32[]{:S(2)}, u32[]{:S(2)}) collective-permute-start(bf16[4,16,64,512]{3,2,1,0:T(8,128)(2,1)} %get-tuple-element.45), channel_id=1, source_target_pairs={{0,1},{1,0},{2,3},{3,2},{4,5},{5,4},{6,7},{7,6}} | collective-permute-start | bytes 12582920 | tf_op jit(solution)/shard_map/ppermute | solution.py:600
  686.6 24.5 %collective-permute-start.7 = (bf16[16,64,512]{2,1,0:T(8,128)(2,1)}, bf16[16,64,512]{2,1,0:T(8,128)(2,1)S(1)}, u32[]{:S(2)}, u32[]{:S(2)}) collective-permute-start(bf16[16,64,512]{2,1,0:T(8,128)(2,1)} %get-tuple-element.46), channel_id=1, source_target_pairs={{0,2},{1,3},{2,0},{3,1},{4,6},{5,7},{6,4},{7,5}} | collective-permute-start | bytes 3145736 | tf_op jit(solution)/shard_map/ppermute | solution.py:597
  686.6 47.6 %collective-permute-start.8 = (bf16[16,64,512]{2,1,0:T(8,128)(2,1)}, bf16[16,64,512]{2,1,0:T(8,128)(2,1)S(1)}, u32[]{:S(2)}, u32[]{:S(2)}) collective-permute-start(bf16[16,64,512]{2,1,0:T(8,128)(2,1)} %get-tuple-element.47), channel_id=1, source_target_pairs={{0,3},{1,2},{2,1},{3,0},{4,7},{5,6},{6,5},{7,4}} | collective-permute-start | bytes 3145736 | tf_op jit(solution)/shard_map/ppermute | solution.py:598
  711.1 23.1 %copy-start = (bf16[16,64,512]{2,1,0:T(8,128)(2,1)}, bf16[16,64,512]{2,1,0:T(8,128)(2,1)S(1)}, u32[]{:S(2)}) copy-start(bf16[16,64,512]{2,1,0:T(8,128)(2,1)S(1)} %collective-permute-done.7.far_ref) | copy-start | bytes 3145732
  734.2 1.0 copy-start.1
